TPU v7x, 32 devices: a whole 2x2x4 slice. The times are simulated.
32 devices in a mesh: rows: 4 (over y, x), keys: 8 (over z, core).
Axes of the slice: x: 2, y: 2, z: 4, core: 2. Of those that a mesh axis runs over, the one named last changes fastest.
Arguments:
- pair_rep: bfloat16 [192, 384, 128], P('rows', 'keys'), may hold values from -6 to 6
- norm_gain: float32 [128], replicated, may hold values from 0.1 to 1.9
- w_query: bfloat16 [128, 128], replicated, may hold values from -0.5 to 0.5
- w_key: bfloat16 [128, 128], replicated, may hold values from -0.5 to 0.5
- w_value: bfloat16 [128, 128], replicated, may hold values from -0.5 to 0.5
- w_gate: bfloat16 [128, 128], replicated, may hold values from -0.5 to 0.5
- w_out: bfloat16 [128, 128], replicated, may hold values from -0.5 to 0.5
- pair_bias: bfloat16 [4, 384, 384], P(None, 'keys', 'rows'), may hold values from -12 to 300
Outputs:
- update: bfloat16 [192, 384, 128], P('rows', 'keys')
All inputs are finite; a program needn't handle non-finite values.
Results may differ from a plain program's by a relative error of at most 0.025.
Values may be sent and summed in bfloat16 or wider, within the bound.
No kernel may reach another device: no remote copies, remote signals or barrier semaphores. Data moves between devices by JAX's collectives and lax.ppermute only.
A program may use at most 128 MiB of HBM per device.

v0:
```python
import jax
import jax.numpy as jnp
from jax import lax
from jax.sharding import PartitionSpec as P

epsilon = 1e-05
block_rows = 8


def normalize(pair_rep, norm_gain):
    values = pair_rep.astype(jnp.float32)
    center = jnp.mean(values, axis=-1, keepdims=True)
    spread = jnp.mean(jnp.square(values - center), axis=-1, keepdims=True)
    return ((values - center) * lax.rsqrt(spread + epsilon) * norm_gain).astype(jnp.bfloat16)


def split_heads(tensor, head_count):
    return tensor.reshape(tensor.shape[:-1] + (head_count, tensor.shape[-1] // head_count))


def blocked(tensor):
    return tensor.reshape((tensor.shape[0] // block_rows, block_rows) + tensor.shape[1:])


def unblocked(tensor):
    return tensor.reshape((tensor.shape[0] * tensor.shape[1],) + tensor.shape[2:])


def absorb(running, query_block, key_block, value_block, bias_piece, head_count):
    highest, totals, summed = running
    logits = (
        jnp.einsum(
            "rjhd,rkhd->rhjk",
            split_heads(query_block, head_count),
            split_heads(key_block, head_count),
            preferred_element_type=jnp.float32,
        )
        + bias_piece.astype(jnp.float32)[None]
    )
    new_highest = jnp.maximum(highest, jnp.max(logits, axis=3))
    shrink = jnp.exp(highest - new_highest)
    powers = jnp.exp(logits - new_highest[..., None])
    totals = totals * shrink + jnp.sum(powers, axis=3)
    summed = summed * jnp.transpose(shrink, (0, 2, 1))[..., None] + jnp.einsum(
        "rhjk,rkhd->rjhd",
        powers.astype(jnp.bfloat16),
        split_heads(value_block, head_count),
        preferred_element_type=jnp.float32,
    )
    return (new_highest, totals, summed)


def body(pair_rep, norm_gain, w_query, w_key, w_value, w_gate, w_out, pair_bias):
    head_count = pair_bias.shape[0]
    inner_width = w_query.shape[1]
    normed = normalize(pair_rep, norm_gain)
    local_rows, local_keys = (normed.shape[0], normed.shape[1])
    queries = (
        jnp.dot(normed, w_query, preferred_element_type=jnp.float32)
        * (inner_width // head_count) ** (-0.5)
    ).astype(jnp.bfloat16)
    gates = jax.nn.sigmoid(jnp.dot(normed, w_gate, preferred_element_type=jnp.float32))
    bias_full = lax.all_gather(pair_bias, "rows", axis=2, tiled=True)
    initial = (
        jnp.full((local_rows, head_count, local_keys), -1e30, jnp.float32),
        jnp.zeros((local_rows, head_count, local_keys), jnp.float32),
        jnp.zeros((local_rows, local_keys, head_count, inner_width // head_count), jnp.float32),
    )
    piece = lax.all_gather(normed, "keys", axis=1, tiled=True)

    def one_block(arrays):
        highest, totals, summed, query_block, input_block = arrays
        key_block = jnp.dot(input_block, w_key, preferred_element_type=jnp.float32).astype(
            jnp.bfloat16
        )
        value_block = jnp.dot(input_block, w_value, preferred_element_type=jnp.float32).astype(
            jnp.bfloat16
        )
        return absorb(
            (highest, totals, summed), query_block, key_block, value_block, bias_full, head_count
        )

    results = lax.map(one_block, tuple((blocked(tensor) for tensor in initial + (queries, piece))))
    highest, totals, summed = tuple((unblocked(tensor) for tensor in results))
    attended = summed / jnp.transpose(totals, (0, 2, 1))[..., None]
    attended = attended.reshape(local_rows, local_keys, inner_width)
    gated = (gates * attended).astype(jnp.bfloat16)
    return jnp.dot(gated, w_out, preferred_element_type=jnp.float32).astype(jnp.bfloat16)


def solution(mesh):
    placed = (P("rows", "keys", None), P(), P(), P(), P(), P(), P(), P(None, "keys", "rows"))
    return jax.shard_map(
        body, mesh=mesh, in_specs=placed, out_specs=P("rows", "keys", None), check_vma=False
    )
```

profile of v0, /device:TPU:0, one launch (start us, length us, event | category | flops | bytes accessed | tf_op | source)
XLA Modules:
  0.0 119.4 jit_solution(9503435875316959290)
XLA Ops:
  6.6 1.5 %convert_reduce_fusion = f32[48,48]{1,0:T(8,128)S(1)} fusion(bf16[48,48,128]{2,1,0:T(8,128)(2,1)} %param.10), kind=kLoop, calls=%fused_computation.26 | loop fusion | flops 587520 | bytes 599040 | tf_op jit(solution)/shard_map/reduce_sum | solution.py:12
  8.1 1.8 %fusion.25 = f32[48,48]{1,0:T(8,128)S(1)} fusion(bf16[48,48,128]{2,1,0:T(8,128)(2,1)} %param.10, f32[48,48]{1,0:T(8,128)S(1)} %broadcast_multiply_fusion), kind=kLoop, calls=%fused_computation.38 | loop fusion | flops 1177344 | bytes 608256 | tf_op jit(solution)/shard_map/reduce_sum | solution.py:13
  9.9 2.2 %fusion.27 = bf16[48,48,128]{2,1,0:T(8,128)(2,1)} fusion(bf16[48,48,128]{2,1,0:T(8,128)(2,1)S(1)} %copy-done.1, f32[128]{0:T(128)} %param.11, f32[48,48]{1,0:T(8,128)S(1)} %add_rsqrt_fusion, f32[48,48]{1,0:T(8,128)S(1)} %broadcast_multiply_fusion), kind=kLoop, calls=%fused_computation.40 | loop fusion | flops 1474560 | bytes 1198592 | tf_op jit(solution)/shard_map/convert_element_type | solution.py:14
  12.4 11.0 %all_gather.7 = bf16[4,48,384]{1,0,2:T(4,128)(2,1)S(1)} all-gather(bf16[4,48,96]{1,0,2:T(4,128)(2,1)S(1)} %copy.25), channel_id=1, replica_groups=mesh['rows'=4,'keys'=8] {'rows'}, dimensions={2}, use_global_device_ids=true | all-gather | bytes 184320 | tf_op jit(solution)/shard_map/all_gather | solution.py:63
  24.1 42.1 %all-gather.2.cloned.1.call-done = bf16[48,384,128]{2,1,0:T(8,128)(2,1)} async-done(((bf16[48,48,128]{2,1,0:T(8,128)(2,1)}), bf16[48,384,128]{2,1,0:T(8,128)(2,1)}) %all-gather.2.cloned.1.call-update) | async-done | bytes 4718608 | tf_op jit(solution)/shard_map/all_gather | solution.py:69
  66.2 37.7 %while.12 = (s32[]{:T(128)}, f32[6,8,4,48]{3,2,1,0:T(4,128)S(1)}, f32[6,8,48,4,32]{2,4,3,1,0:T(8,128)}, bf16[6,8,48,128]{3,2,1,0:T(8,128)(2,1)S(1)}, bf16[6,8,38...) while((s32[]{:T(128)}, f32[6,8,4,48]{3,2,1,0:T(4,128)S(1)}, ...), condition=%wide.region_5.6_spmd, body=%wide.region_2.5_spmd.sunk | while | flops 282459648 | bytes 14303353 | solution.py:83
  66.4 1.5 %convolution_convert_fusion.5 = bf16[8,384,128]{1,2,0:T(8,128)(2,1)S(1)} fusion(bf16[6,8,384,128]{3,2,1,0:T(8,128)(2,1)} %get-tuple-element.181, s32[]{:T(128)S(6)} %copy.40, bf16[128,128]{0,1:T(8,128)(2,1)S(1)} %get-tuple-element.182), kind=kOutput, calls=%fused_computation.5.clone.1 | convolution fusion | flops 101056512 | bytes 1605636 | tf_op jit(solution)/shard_map/while/body/eval_jaxpr/dot_general | solution.py:73
  68.6 0.8 fusion.60
  69.5 1.5 %convolution_convert_fusion.6 = bf16[8,384,128]{1,2,0:T(8,128)(2,1)S(1)} fusion(bf16[6,8,384,128]{3,2,1,0:T(8,128)(2,1)} %get-tuple-element.181, s32[]{:T(128)S(6)} %copy.40, bf16[128,128]{0,1:T(8,128)(2,1)S(1)} %get-tuple-element.184), kind=kOutput, calls=%fused_computation.4.clone.1 | convolution fusion | flops 101056512 | bytes 1605636 | tf_op jit(solution)/shard_map/while/body/eval_jaxpr/dot_general | solution.py:76
  71.0 1.5 %fusion.61 = f32[6,8,48,4,32]{2,4,3,1,0:T(8,128)} fusion(f32[6,8,48,4,32]{2,4,3,1,0:T(8,128)} %get-tuple-element.170, s32[]{:T(128)S(6)} %copy.40, bf16[8,384,4,32]{1,3,2,0:T(8,128)(2,1)S(1)} %bitcast.81, f32[8,4,48,384]{3,2,1,0:T(8,128)S(1)} %get-tuple-element.155, f32[8,4,48]{2,1,0:T(4,128)S(1)} %get-tuple-element.157, ...), kind=kOutput, calls=%fused_computation.9.clone.1 | convolution fusion | flops 39567360 | bytes 3977220 | tf_op jit(solution)/shard_map/while/body/eval_jaxpr/rhjk,rkhd->rjhd/dot_general | solution.py:44
  72.7 1.5 %convolution_convert_fusion.5 = bf16[8,384,128]{1,2,0:T(8,128)(2,1)S(1)} fusion(bf16[6,8,384,128]{3,2,1,0:T(8,128)(2,1)} %get-tuple-element.181, s32[]{:T(128)S(6)} %copy.40, bf16[128,128]{0,1:T(8,128)(2,1)S(1)} %get-tuple-element.182), kind=kOutput, calls=%fused_computation.5.clone.1 | convolution fusion | flops 101056512 | bytes 1605636 | tf_op jit(solution)/shard_map/while/body/eval_jaxpr/dot_general | solution.py:73
  74.9 0.8 fusion.60
  75.8 1.5 %convolution_convert_fusion.6 = bf16[8,384,128]{1,2,0:T(8,128)(2,1)S(1)} fusion(bf16[6,8,384,128]{3,2,1,0:T(8,128)(2,1)} %get-tuple-element.181, s32[]{:T(128)S(6)} %copy.40, bf16[128,128]{0,1:T(8,128)(2,1)S(1)} %get-tuple-element.184), kind=kOutput, calls=%fused_computation.4.clone.1 | convolution fusion | flops 101056512 | bytes 1605636 | tf_op jit(solution)/shard_map/while/body/eval_jaxpr/dot_general | solution.py:76
  77.3 1.5 %fusion.61 = f32[6,8,48,4,32]{2,4,3,1,0:T(8,128)} fusion(f32[6,8,48,4,32]{2,4,3,1,0:T(8,128)} %get-tuple-element.170, s32[]{:T(128)S(6)} %copy.40, bf16[8,384,4,32]{1,3,2,0:T(8,128)(2,1)S(1)} %bitcast.81, f32[8,4,48,384]{3,2,1,0:T(8,128)S(1)} %get-tuple-element.155, f32[8,4,48]{2,1,0:T(4,128)S(1)} %get-tuple-element.157, ...), kind=kOutput, calls=%fused_computation.9.clone.1 | convolution fusion | flops 39567360 | bytes 3977220 | tf_op jit(solution)/shard_map/while/body/eval_jaxpr/rhjk,rkhd->rjhd/dot_general | solution.py:44
  79.0 1.5 %convolution_convert_fusion.5 = bf16[8,384,128]{1,2,0:T(8,128)(2,1)S(1)} fusion(bf16[6,8,384,128]{3,2,1,0:T(8,128)(2,1)} %get-tuple-element.181, s32[]{:T(128)S(6)} %copy.40, bf16[128,128]{0,1:T(8,128)(2,1)S(1)} %get-tuple-element.182), kind=kOutput, calls=%fused_computation.5.clone.1 | convolution fusion | flops 101056512 | bytes 1605636 | tf_op jit(solution)/shard_map/while/body/eval_jaxpr/dot_general | solution.py:73
  81.2 0.8 fusion.60
  82.1 1.5 %convolution_convert_fusion.6 = bf16[8,384,128]{1,2,0:T(8,128)(2,1)S(1)} fusion(bf16[6,8,384,128]{3,2,1,0:T(8,128)(2,1)} %get-tuple-element.181, s32[]{:T(128)S(6)} %copy.40, bf16[128,128]{0,1:T(8,128)(2,1)S(1)} %get-tuple-element.184), kind=kOutput, calls=%fused_computation.4.clone.1 | convolution fusion | flops 101056512 | bytes 1605636 | tf_op jit(solution)/shard_map/while/body/eval_jaxpr/dot_general | solution.py:76
  83.6 1.5 %fusion.61 = f32[6,8,48,4,32]{2,4,3,1,0:T(8,128)} fusion(f32[6,8,48,4,32]{2,4,3,1,0:T(8,128)} %get-tuple-element.170, s32[]{:T(128)S(6)} %copy.40, bf16[8,384,4,32]{1,3,2,0:T(8,128)(2,1)S(1)} %bitcast.81, f32[8,4,48,384]{3,2,1,0:T(8,128)S(1)} %get-tuple-element.155, f32[8,4,48]{2,1,0:T(4,128)S(1)} %get-tuple-element.157, ...), kind=kOutput, calls=%fused_computation.9.clone.1 | convolution fusion | flops 39567360 | bytes 3977220 | tf_op jit(solution)/shard_map/while/body/eval_jaxpr/rhjk,rkhd->rjhd/dot_general | solution.py:44
  85.3 1.5 %convolution_convert_fusion.5 = bf16[8,384,128]{1,2,0:T(8,128)(2,1)S(1)} fusion(bf16[6,8,384,128]{3,2,1,0:T(8,128)(2,1)} %get-tuple-element.181, s32[]{:T(128)S(6)} %copy.40, bf16[128,128]{0,1:T(8,128)(2,1)S(1)} %get-tuple-element.182), kind=kOutput, calls=%fused_computation.5.clone.1 | convolution fusion | flops 101056512 | bytes 1605636 | tf_op jit(solution)/shard_map/while/body/eval_jaxpr/dot_general | solution.py:73
  87.5 0.8 fusion.60
  88.3 1.5 %convolution_convert_fusion.6 = bf16[8,384,128]{1,2,0:T(8,128)(2,1)S(1)} fusion(bf16[6,8,384,128]{3,2,1,0:T(8,128)(2,1)} %get-tuple-element.181, s32[]{:T(128)S(6)} %copy.40, bf16[128,128]{0,1:T(8,128)(2,1)S(1)} %get-tuple-element.184), kind=kOutput, calls=%fused_computation.4.clone.1 | convolution fusion | flops 101056512 | bytes 1605636 | tf_op jit(solution)/shard_map/while/body/eval_jaxpr/dot_general | solution.py:76
  89.9 1.5 %fusion.61 = f32[6,8,48,4,32]{2,4,3,1,0:T(8,128)} fusion(f32[6,8,48,4,32]{2,4,3,1,0:T(8,128)} %get-tuple-element.170, s32[]{:T(128)S(6)} %copy.40, bf16[8,384,4,32]{1,3,2,0:T(8,128)(2,1)S(1)} %bitcast.81, f32[8,4,48,384]{3,2,1,0:T(8,128)S(1)} %get-tuple-element.155, f32[8,4,48]{2,1,0:T(4,128)S(1)} %get-tuple-element.157, ...), kind=kOutput, calls=%fused_computation.9.clone.1 | convolution fusion | flops 39567360 | bytes 3977220 | tf_op jit(solution)/shard_map/while/body/eval_jaxpr/rhjk,rkhd->rjhd/dot_general | solution.py:44
  91.6 1.5 %convolution_convert_fusion.5 = bf16[8,384,128]{1,2,0:T(8,128)(2,1)S(1)} fusion(bf16[6,8,384,128]{3,2,1,0:T(8,128)(2,1)} %get-tuple-element.181, s32[]{:T(128)S(6)} %copy.40, bf16[128,128]{0,1:T(8,128)(2,1)S(1)} %get-tuple-element.182), kind=kOutput, calls=%fused_computation.5.clone.1 | convolution fusion | flops 101056512 | bytes 1605636 | tf_op jit(solution)/shard_map/while/body/eval_jaxpr/dot_general | solution.py:73
  93.7 0.8 fusion.60
  94.6 1.5 %convolution_convert_fusion.6 = bf16[8,384,128]{1,2,0:T(8,128)(2,1)S(1)} fusion(bf16[6,8,384,128]{3,2,1,0:T(8,128)(2,1)} %get-tuple-element.181, s32[]{:T(128)S(6)} %copy.40, bf16[128,128]{0,1:T(8,128)(2,1)S(1)} %get-tuple-element.184), kind=kOutput, calls=%fused_computation.4.clone.1 | convolution fusion | flops 101056512 | bytes 1605636 | tf_op jit(solution)/shard_map/while/body/eval_jaxpr/dot_general | solution.py:76
  96.1 1.5 %fusion.61 = f32[6,8,48,4,32]{2,4,3,1,0:T(8,128)} fusion(f32[6,8,48,4,32]{2,4,3,1,0:T(8,128)} %get-tuple-element.170, s32[]{:T(128)S(6)} %copy.40, bf16[8,384,4,32]{1,3,2,0:T(8,128)(2,1)S(1)} %bitcast.81, f32[8,4,48,384]{3,2,1,0:T(8,128)S(1)} %get-tuple-element.155, f32[8,4,48]{2,1,0:T(4,128)S(1)} %get-tuple-element.157, ...), kind=kOutput, calls=%fused_computation.9.clone.1 | convolution fusion | flops 39567360 | bytes 3977220 | tf_op jit(solution)/shard_map/while/body/eval_jaxpr/rhjk,rkhd->rjhd/dot_general | solution.py:44
  97.9 1.5 %convolution_convert_fusion.5 = bf16[8,384,128]{1,2,0:T(8,128)(2,1)S(1)} fusion(bf16[6,8,384,128]{3,2,1,0:T(8,128)(2,1)} %get-tuple-element.181, s32[]{:T(128)S(6)} %copy.40, bf16[128,128]{0,1:T(8,128)(2,1)S(1)} %get-tuple-element.182), kind=kOutput, calls=%fused_computation.5.clone.1 | convolution fusion | flops 101056512 | bytes 1605636 | tf_op jit(solution)/shard_map/while/body/eval_jaxpr/dot_general | solution.py:73
  100.9 1.5 %convolution_convert_fusion.6 = bf16[8,384,128]{1,2,0:T(8,128)(2,1)S(1)} fusion(bf16[6,8,384,128]{3,2,1,0:T(8,128)(2,1)} %get-tuple-element.181, s32[]{:T(128)S(6)} %copy.40, bf16[128,128]{0,1:T(8,128)(2,1)S(1)} %get-tuple-element.184), kind=kOutput, calls=%fused_computation.4.clone.1 | convolution fusion | flops 101056512 | bytes 1605636 | tf_op jit(solution)/shard_map/while/body/eval_jaxpr/dot_general | solution.py:76
  102.4 1.5 %fusion.61 = f32[6,8,48,4,32]{2,4,3,1,0:T(8,128)} fusion(f32[6,8,48,4,32]{2,4,3,1,0:T(8,128)} %get-tuple-element.170, s32[]{:T(128)S(6)} %copy.40, bf16[8,384,4,32]{1,3,2,0:T(8,128)(2,1)S(1)} %bitcast.81, f32[8,4,48,384]{3,2,1,0:T(8,128)S(1)} %get-tuple-element.155, f32[8,4,48]{2,1,0:T(4,128)S(1)} %get-tuple-element.157, ...), kind=kOutput, calls=%fused_computation.9.clone.1 | convolution fusion | flops 39567360 | bytes 3977220 | tf_op jit(solution)/shard_map/while/body/eval_jaxpr/rhjk,rkhd->rjhd/dot_general | solution.py:44
  103.9 3.1 %copy.30 = f32[48,48,128]{2,1,0:T(8,128)} copy(f32[48,48,128]{1,2,0:T(8,128)} %bitcast.85) | data formatting | bytes 2359296 | tf_op jit(solution)/shard_map/reshape | solution.py:26
  107.3 2.0 %copy.31 = f32[48,48,128]{2,1,0:T(8,128)} copy(f32[48,48,128]{1,2,0:T(8,128)S(1)} %bitcast.84) | data formatting | bytes 2359296 | tf_op jit(solution)/shard_map/div | solution.py:85
  109.3 3.3 %convolution_convert_fusion.2 = bf16[48,48,128]{2,1,0:T(8,128)(2,1)} fusion(bf16[48,48,128]{2,1,0:T(8,128)(2,1)} %fusion.27, f32[48,48,128]{2,1,0:T(8,128)} %copy.30, f32[48,48,128]{2,1,0:T(8,128)} %copy.31, bf16[128,128]{1,0:T(8,128)(2,1)S(1)} %copy-done.6, bf16[128,128]{1,0:T(8,128)(2,1)S(1)} %copy-done.7), kind=kOutput, calls=%fused_computation.37 | convolution fusion | flops 153059328 | bytes 3604480 | tf_op jit(solution)/shard_map/dot_general | solution.py:88
  (65 shorter events, 7.3 us)
Async XLA Ops:
  6.5 17.2 %copy-start = (bf16[128,128]{1,0:T(8,128)(2,1)S(1)}, bf16[128,128]{1,0:T(8,128)(2,1)}, u32[]{:S(2)}) copy-start(bf16[128,128]{1,0:T(8,128)(2,1)} %param.12) | copy-start | bytes 98308
  6.5 3.4 %copy-start.1 = (bf16[48,48,128]{2,1,0:T(8,128)(2,1)S(1)}, bf16[48,48,128]{2,1,0:T(8,128)(2,1)}, u32[]{:S(2)}) copy-start(bf16[48,48,128]{2,1,0:T(8,128)(2,1)} %param.10) | copy-start | bytes 1769476
  6.5 5.6 %copy-start.4 = (bf16[128,128]{1,0:T(8,128)(2,1)S(1)}, bf16[128,128]{1,0:T(8,128)(2,1)}, u32[]{:S(2)}) copy-start(bf16[128,128]{1,0:T(8,128)(2,1)} %param.13) | copy-start | bytes 98308
  6.5 5.7 %copy-start.3 = (bf16[4,48,96]{2,1,0:T(8,128)(2,1)S(1)}, bf16[4,48,96]{2,1,0:T(8,128)(2,1)}, u32[]{:S(2)}) copy-start(bf16[4,48,96]{2,1,0:T(8,128)(2,1)} %param.17) | copy-start | bytes 110596
  6.5 59.7 %all-gather.2.cloned.1.call-start = ((), (), s32[]{:S(2)}) async-start(), calls=%async_computation | async-start | bytes 5308416 | tf_op jit(solution)/shard_map/all_gather | solution.py:69
  9.9 13.8 %copy-start.5 = (bf16[128,128]{1,0:T(8,128)(2,1)S(1)}, bf16[128,128]{1,0:T(8,128)(2,1)}, u32[]{:S(2)}) copy-start(bf16[128,128]{1,0:T(8,128)(2,1)} %param.14) | copy-start | bytes 98308
  12.1 11.7 %copy-start.2 = (bf16[48,48,128]{2,1,0:T(8,128)(2,1)S(1)}, bf16[48,48,128]{2,1,0:T(8,128)(2,1)}, u32[]{:S(2)}) copy-start(bf16[48,48,128]{2,1,0:T(8,128)(2,1)} %fusion.27) | copy-start | bytes 1769476
  107.3 2.0 %copy-start.6 = (bf16[128,128]{1,0:T(8,128)(2,1)S(1)}, bf16[128,128]{1,0:T(8,128)(2,1)}, u32[]{:S(2)}) copy-start(bf16[128,128]{1,0:T(8,128)(2,1)} %param.16) | copy-start | bytes 98308
  107.3 2.0 %copy-start.7 = (bf16[128,128]{1,0:T(8,128)(2,1)S(1)}, bf16[128,128]{1,0:T(8,128)(2,1)}, u32[]{:S(2)}) copy-start(bf16[128,128]{1,0:T(8,128)(2,1)} %param.15) | copy-start | bytes 98308
Sparse Core Ops, SparseCore 0:
  12.2 53.9 all-gather.1
where the time goes:
time: 120 us; the launch traced here: 119 us
  waiting for transfers between devices  42.1 us (35%)
  matrix products  34.4 us (29%)
  between operations  13.6 us (11%)
  blocking collectives  11 us (9%)
  other arithmetic  10.9 us (9%)
  local copies, waits for them, and re-layouts  7.1 us (6%)
    all_gather x1, waiting for transfers between devices, body(): piece = lax.all_gather(normed, 'keys', axis=1, tiled=True)  42.1 us
    all_gather x1, blocking collectives, body(): bias_full = lax.all_gather(pair_bias, 'rows', axis=2, tiled=True)  11 us
    dot_general x6, matrix products, absorb(): jnp.einsum('rhjk,rkhd->rjhd', powers.astype(jnp.bfloat16), split_heads(va...  9.1 us
    dot_general x6, matrix products, one_block(): jnp.dot(input_block, w_value, preferred_element_type=jnp.float32)  9.03 us
    dot_general x6, matrix products, one_block(): jnp.dot(input_block, w_key, preferred_element_type=jnp.float32)  9.02 us
    reduce_sum x6, other arithmetic, absorb(): totals = totals * shrink + jnp.sum(powers, axis=3)  5.06 us
    dot_general x6, matrix products, absorb(): jnp.einsum('rjhd,rkhd->rhjk', split_heads(query_block, head_count), split...  3.65 us
    dot_general x1, matrix products, body(): jnp.dot(gated, w_out, preferred_element_type=jnp.float32)  3.32 us
  transfers between devices with their start and end apart: 1, of which 1 were waited for; matrix products, arithmetic and copies ran while one was open for 1% of the time, Pallas kernels for 0%

commit v1 on v0

--- a/solution.py
+++ b/solution.py
@@ -66,7 +66,12 @@
         jnp.zeros((local_rows, head_count, local_keys), jnp.float32),
         jnp.zeros((local_rows, local_keys, head_count, inner_width // head_count), jnp.float32),
     )
-    piece = lax.all_gather(normed, "keys", axis=1, tiled=True)
+    ring = [normed]
+    for hop in range(7):
+        ring.append(lax.ppermute(ring[-1], "keys", [(dev, (dev + 1) % 8) for dev in range(8)]))
+    piece = jnp.roll(
+        jnp.concatenate(ring[::-1], axis=1), (lax.axis_index("keys") + 1) * ring[0].shape[1], axis=1
+    )
 
     def one_block(arrays):
         highest, totals, summed, query_block, input_block = arrays

time: 120 us -> 150 us (1.25)
  waiting for transfers between devices: 42.1 us -> 67.2 us
  local copies, waits for them, and re-layouts: 7.1 us -> 24.9 us
  between operations: 13.6 us -> 0.33 us
  other arithmetic: 10.9 us -> 12.5 us
    ppermute x0 -> x7, waiting for transfers between devices: none -> 67.2 us  [body(): lax.ppermute(ring[-1], 'keys', [(dev, (dev + 1) % 8) for dev in range(8)])]
    all_gather x1 -> x0, waiting for transfers between devices: 42.1 us -> none  [body(): piece = lax.all_gather(normed, 'keys', axis=1, tiled=True)]
    unnamed x17 -> x43, local copies, waits for them, and re-layouts: 0.16 us -> 7.64 us
    dynamic_slice x12, local copies, waits for them, and re-layouts: 1.17 us -> 6.5 us  [body(): lax.map(one_block, tuple((blocked(tensor) for tensor in initial + (querie...]
    dynamic_slice x0 -> x1, local copies, waits for them, and re-layouts: none -> 4.18 us  [body(): jnp.roll(jnp.concatenate(ring[::-1], axis=1), (lax.axis_index('keys') + 1...]
    dot_general x1, matrix products: 3.32 us -> 1.52 us  [body(): jnp.dot(gated, w_out, preferred_element_type=jnp.float32)]
    while x3, local copies, waits for them, and re-layouts: 0.46 us -> 1.98 us  [body(): lax.map(one_block, tuple((blocked(tensor) for tensor in initial + (querie...]
  transfers between devices with their start and end apart: 1 -> 7, of which waited for: 1 -> 6; matrix products, arithmetic and copies ran while one was open for 1% -> 2% of each run, Pallas kernels for 0% -> 0%
where the time goes in v1:
time: 150 us; the launch traced here: 149 us
  waiting for transfers between devices  67.2 us (45%)
  matrix products  33.2 us (22%)
  local copies, waits for them, and re-layouts  24.9 us (17%)
  other arithmetic  12.5 us (8%)
  blocking collectives  10 us (7%)
    ppermute x7, waiting for transfers between devices, body(): lax.ppermute(ring[-1], 'keys', [(dev, (dev + 1) % 8) for dev in range(8)])  67.2 us
    all_gather x1, blocking collectives, body(): bias_full = lax.all_gather(pair_bias, 'rows', axis=2, tiled=True)  10 us
    dot_general x6, matrix products, one_block(): jnp.dot(input_block, w_value, preferred_element_type=jnp.float32)  9.02 us
    dot_general x6, matrix products, one_block(): jnp.dot(input_block, w_key, preferred_element_type=jnp.float32)  9.01 us
    dot_general x6, matrix products, absorb(): jnp.einsum('rhjk,rkhd->rjhd', powers.astype(jnp.bfloat16), split_heads(va...  8.8 us
    unnamed x43, local copies, waits for them, and re-layouts  7.64 us
    dynamic_slice x12, local copies, waits for them, and re-layouts, body(): lax.map(one_block, tuple((blocked(tensor) for tensor in initial + (querie...  6.5 us
    reduce_sum x6, other arithmetic, absorb(): totals = totals * shrink + jnp.sum(powers, axis=3)  5.06 us
  transfers between devices with their start and end apart: 7, of which 6 were waited for; matrix products, arithmetic and copies ran while one was open for 2% of the time, Pallas kernels for 0%

profile of v1, /device:TPU:0, one launch (start us, length us, event | category | flops | bytes accessed | tf_op | source)
XLA Modules:
  0.0 149.1 jit_solution(3848878565944393177)
XLA Ops:
  0.0 1.5 convert_reduce_fusion
  1.5 1.8 %fusion.25 = f32[48,48]{1,0:T(8,128)S(1)} fusion(bf16[48,48,128]{2,1,0:T(8,128)(2,1)} %param.10, f32[48,48]{1,0:T(8,128)S(1)} %broadcast_multiply_fusion), kind=kLoop, calls=%fused_computation.38 | loop fusion | flops 1177344 | bytes 608256 | tf_op jit(solution)/shard_map/reduce_sum | solution.py:13
  3.9 1.7 %fusion.27 = bf16[48,48,128]{2,1,0:T(8,128)(2,1)S(1)} fusion(bf16[48,48,128]{2,1,0:T(8,128)(2,1)} %param.10, f32[128]{0:T(128)} %param.11, f32[48,48]{1,0:T(8,128)S(1)} %add_rsqrt_fusion, f32[48,48]{1,0:T(8,128)S(1)} %broadcast_multiply_fusion), kind=kLoop, calls=%fused_computation.40 | loop fusion | flops 1474560 | bytes 1198592 | tf_op jit(solution)/shard_map/convert_element_type | solution.py:14
  6.2 11.6 %collective-permute-done = bf16[48,48,128]{2,1,0:T(8,128)(2,1)S(1)} collective-permute-done((bf16[48,48,128]{2,1,0:T(8,128)(2,1)S(1)}, bf16[48,48,128]{2,1,0:T(8,128)(2,1)S(1)}, u32[]{:S(2)}, u32[]{:S(2)}) %collective-permute-start) | collective-permute-done | bytes 589856 | tf_op jit(solution)/shard_map/ppermute | solution.py:71
  17.8 11.1 %collective-permute-done.1 = bf16[48,48,128]{2,1,0:T(8,128)(2,1)S(1)} collective-permute-done((bf16[48,48,128]{2,1,0:T(8,128)(2,1)S(1)}, bf16[48,48,128]{2,1,0:T(8,128)(2,1)S(1)}, u32[]{:S(2)}, u32[]{:S(2)}) %collective-permute-start.1) | collective-permute-done | bytes 589856 | tf_op jit(solution)/shard_map/ppermute | solution.py:71
  28.9 11.1 %collective-permute-done.2 = bf16[48,48,128]{2,1,0:T(8,128)(2,1)S(1)} collective-permute-done((bf16[48,48,128]{2,1,0:T(8,128)(2,1)S(1)}, bf16[48,48,128]{2,1,0:T(8,128)(2,1)S(1)}, u32[]{:S(2)}, u32[]{:S(2)}) %collective-permute-start.2) | collective-permute-done | bytes 589856 | tf_op jit(solution)/shard_map/ppermute | solution.py:71
  40.0 11.1 %collective-permute-done.3 = bf16[48,48,128]{2,1,0:T(8,128)(2,1)S(1)} collective-permute-done((bf16[48,48,128]{2,1,0:T(8,128)(2,1)S(1)}, bf16[48,48,128]{2,1,0:T(8,128)(2,1)S(1)}, u32[]{:S(2)}, u32[]{:S(2)}) %collective-permute-start.3) | collective-permute-done | bytes 589856 | tf_op jit(solution)/shard_map/ppermute | solution.py:71
  51.1 11.1 %collective-permute-done.4 = bf16[48,48,128]{2,1,0:T(8,128)(2,1)S(1)} collective-permute-done((bf16[48,48,128]{2,1,0:T(8,128)(2,1)S(1)}, bf16[48,48,128]{2,1,0:T(8,128)(2,1)S(1)}, u32[]{:S(2)}, u32[]{:S(2)}) %collective-permute-start.4) | collective-permute-done | bytes 589856 | tf_op jit(solution)/shard_map/ppermute | solution.py:71
  63.0 11.2 %collective-permute-done.5 = bf16[48,48,128]{2,1,0:T(8,128)(2,1)} collective-permute-done((bf16[48,48,128]{2,1,0:T(8,128)(2,1)S(1)}, bf16[48,48,128]{2,1,0:T(8,128)(2,1)}, u32[]{:S(2)}, u32[]{:S(2)}) %collective-permute-start.5) | collective-permute-done | bytes 589856 | tf_op jit(solution)/shard_map/ppermute | solution.py:71
  74.4 10.0 %all_gather.3 = bf16[4,48,384]{1,0,2:T(4,128)(2,1)S(1)} all-gather(bf16[4,48,96]{1,0,2:T(4,128)(2,1)S(1)} %copy.25), channel_id=1, replica_groups=mesh['rows'=4,'keys'=8] {'rows'}, dimensions={2}, use_global_device_ids=true | all-gather | bytes 184320 | tf_op jit(solution)/shard_map/all_gather | solution.py:63
  95.8 4.2 %constant_dynamic-slice_fusion.1 = bf16[48,384,128]{2,1,0:T(8,128)(2,1)} fusion(bf16[48,768,128]{2,1,0:T(8,128)(2,1)S(1)} %constant_dynamic-update-slice_fusion, s32[]{:T(128)S(6)} %select_n.14), kind=kLoop, calls=%fused_computation.64 | loop fusion | bytes 9437188 | tf_op jit(solution)/shard_map/jit(_roll_dynamic)/dynamic_slice | solution.py:72
  100.0 42.8 %while.12 = (s32[]{:T(128)}, f32[6,8,4,48]{3,2,1,0:T(4,128)S(1)}, f32[6,8,48,4,32]{2,4,3,1,0:T(8,128)}, bf16[6,8,48,128]{3,2,1,0:T(8,128)(2,1)}, bf16[6,8,384,12...) while((s32[]{:T(128)}, f32[6,8,4,48]{3,2,1,0:T(4,128)S(1)}, ...), condition=%wide.region_5.6_spmd, body=%wide.region_2.5_spmd.sunk | while | flops 282459648 | bytes 14304869 | solution.py:88
  100.0 1.5 %convolution_convert_fusion.5 = bf16[8,384,128]{1,2,0:T(8,128)(2,1)S(1)} fusion(bf16[6,8,384,128]{3,2,1,0:T(8,128)(2,1)} %get-tuple-element.181, s32[]{:T(128)} %get-tuple-element.168, bf16[128,128]{0,1:T(8,128)(2,1)S(1)} %get-tuple-element.182), kind=kOutput, calls=%fused_computation.5.clone.1 | convolution fusion | flops 101056512 | bytes 1606144 | tf_op jit(solution)/shard_map/while/body/eval_jaxpr/dot_general | solution.py:78
  103.3 1.5 %convolution_convert_fusion.6 = bf16[8,384,128]{1,2,0:T(8,128)(2,1)S(1)} fusion(bf16[6,8,384,128]{3,2,1,0:T(8,128)(2,1)} %get-tuple-element.181, s32[]{:T(128)} %get-tuple-element.168, bf16[128,128]{0,1:T(8,128)(2,1)S(1)} %get-tuple-element.184), kind=kOutput, calls=%fused_computation.4.clone.1 | convolution fusion | flops 101056512 | bytes 1606144 | tf_op jit(solution)/shard_map/while/body/eval_jaxpr/dot_general | solution.py:81
  104.8 1.5 fusion.61
  107.2 1.5 %convolution_convert_fusion.5 = bf16[8,384,128]{1,2,0:T(8,128)(2,1)S(1)} fusion(bf16[6,8,384,128]{3,2,1,0:T(8,128)(2,1)} %get-tuple-element.181, s32[]{:T(128)} %get-tuple-element.168, bf16[128,128]{0,1:T(8,128)(2,1)S(1)} %get-tuple-element.182), kind=kOutput, calls=%fused_computation.5.clone.1 | convolution fusion | flops 101056512 | bytes 1606144 | tf_op jit(solution)/shard_map/while/body/eval_jaxpr/dot_general | solution.py:78
  110.4 1.5 %convolution_convert_fusion.6 = bf16[8,384,128]{1,2,0:T(8,128)(2,1)S(1)} fusion(bf16[6,8,384,128]{3,2,1,0:T(8,128)(2,1)} %get-tuple-element.181, s32[]{:T(128)} %get-tuple-element.168, bf16[128,128]{0,1:T(8,128)(2,1)S(1)} %get-tuple-element.184), kind=kOutput, calls=%fused_computation.4.clone.1 | convolution fusion | flops 101056512 | bytes 1606144 | tf_op jit(solution)/shard_map/while/body/eval_jaxpr/dot_general | solution.py:81
  111.9 1.5 %fusion.61 = f32[6,8,48,4,32]{2,4,3,1,0:T(8,128)} fusion(f32[6,8,48,4,32]{2,4,3,1,0:T(8,128)} %get-tuple-element.170, s32[]{:T(128)} %get-tuple-element.168, bf16[8,384,4,32]{1,3,2,0:T(8,128)(2,1)S(1)} %bitcast.81, f32[8,4,48,384]{3,2,1,0:T(8,128)S(1)} %get-tuple-element.155, f32[8,4,48]{2,1,0:T(4,128)S(1)} %get-tuple-element.157, ...), kind=kOutput, calls=%fused_computation.9.clone.1 | convolution fusion | flops 39567360 | bytes 3977728 | tf_op jit(solution)/shard_map/while/body/eval_jaxpr/rhjk,rkhd->rjhd/dot_general | solution.py:44
  114.3 1.5 %convolution_convert_fusion.5 = bf16[8,384,128]{1,2,0:T(8,128)(2,1)S(1)} fusion(bf16[6,8,384,128]{3,2,1,0:T(8,128)(2,1)} %get-tuple-element.181, s32[]{:T(128)} %get-tuple-element.168, bf16[128,128]{0,1:T(8,128)(2,1)S(1)} %get-tuple-element.182), kind=kOutput, calls=%fused_computation.5.clone.1 | convolution fusion | flops 101056512 | bytes 1606144 | tf_op jit(solution)/shard_map/while/body/eval_jaxpr/dot_general | solution.py:78
  117.6 1.5 %convolution_convert_fusion.6 = bf16[8,384,128]{1,2,0:T(8,128)(2,1)S(1)} fusion(bf16[6,8,384,128]{3,2,1,0:T(8,128)(2,1)} %get-tuple-element.181, s32[]{:T(128)} %get-tuple-element.168, bf16[128,128]{0,1:T(8,128)(2,1)S(1)} %get-tuple-element.184), kind=kOutput, calls=%fused_computation.4.clone.1 | convolution fusion | flops 101056512 | bytes 1606144 | tf_op jit(solution)/shard_map/while/body/eval_jaxpr/dot_general | solution.py:81
  119.1 1.5 fusion.61
  121.5 1.5 %convolution_convert_fusion.5 = bf16[8,384,128]{1,2,0:T(8,128)(2,1)S(1)} fusion(bf16[6,8,384,128]{3,2,1,0:T(8,128)(2,1)} %get-tuple-element.181, s32[]{:T(128)} %get-tuple-element.168, bf16[128,128]{0,1:T(8,128)(2,1)S(1)} %get-tuple-element.182), kind=kOutput, calls=%fused_computation.5.clone.1 | convolution fusion | flops 101056512 | bytes 1606144 | tf_op jit(solution)/shard_map/while/body/eval_jaxpr/dot_general | solution.py:78
  124.7 1.5 %convolution_convert_fusion.6 = bf16[8,384,128]{1,2,0:T(8,128)(2,1)S(1)} fusion(bf16[6,8,384,128]{3,2,1,0:T(8,128)(2,1)} %get-tuple-element.181, s32[]{:T(128)} %get-tuple-element.168, bf16[128,128]{0,1:T(8,128)(2,1)S(1)} %get-tuple-element.184), kind=kOutput, calls=%fused_computation.4.clone.1 | convolution fusion | flops 101056512 | bytes 1606144 | tf_op jit(solution)/shard_map/while/body/eval_jaxpr/dot_general | solution.py:81
  126.3 1.5 fusion.61
  128.6 1.5 %convolution_convert_fusion.5 = bf16[8,384,128]{1,2,0:T(8,128)(2,1)S(1)} fusion(bf16[6,8,384,128]{3,2,1,0:T(8,128)(2,1)} %get-tuple-element.181, s32[]{:T(128)} %get-tuple-element.168, bf16[128,128]{0,1:T(8,128)(2,1)S(1)} %get-tuple-element.182), kind=kOutput, calls=%fused_computation.5.clone.1 | convolution fusion | flops 101056512 | bytes 1606144 | tf_op jit(solution)/shard_map/while/body/eval_jaxpr/dot_general | solution.py:78
  131.9 1.5 %convolution_convert_fusion.6 = bf16[8,384,128]{1,2,0:T(8,128)(2,1)S(1)} fusion(bf16[6,8,384,128]{3,2,1,0:T(8,128)(2,1)} %get-tuple-element.181, s32[]{:T(128)} %get-tuple-element.168, bf16[128,128]{0,1:T(8,128)(2,1)S(1)} %get-tuple-element.184), kind=kOutput, calls=%fused_computation.4.clone.1 | convolution fusion | flops 101056512 | bytes 1606144 | tf_op jit(solution)/shard_map/while/body/eval_jaxpr/dot_general | solution.py:81
  135.7 1.5 %convolution_convert_fusion.5 = bf16[8,384,128]{1,2,0:T(8,128)(2,1)S(1)} fusion(bf16[6,8,384,128]{3,2,1,0:T(8,128)(2,1)} %get-tuple-element.181, s32[]{:T(128)} %get-tuple-element.168, bf16[128,128]{0,1:T(8,128)(2,1)S(1)} %get-tuple-element.182), kind=kOutput, calls=%fused_computation.5.clone.1 | convolution fusion | flops 101056512 | bytes 1606144 | tf_op jit(solution)/shard_map/while/body/eval_jaxpr/dot_general | solution.py:78
  139.0 1.5 %convolution_convert_fusion.6 = bf16[8,384,128]{1,2,0:T(8,128)(2,1)S(1)} fusion(bf16[6,8,384,128]{3,2,1,0:T(8,128)(2,1)} %get-tuple-element.181, s32[]{:T(128)} %get-tuple-element.168, bf16[128,128]{0,1:T(8,128)(2,1)S(1)} %get-tuple-element.184), kind=kOutput, calls=%fused_computation.4.clone.1 | convolution fusion | flops 101056512 | bytes 1606144 | tf_op jit(solution)/shard_map/while/body/eval_jaxpr/dot_general | solution.py:81
  140.5 1.5 fusion.61
  143.1 2.0 %copy.31 = f32[48,48,128]{2,1,0:T(8,128)} copy(f32[48,48,128]{1,2,0:T(8,128)S(1)} %bitcast.84) | data formatting | bytes 2359296 | tf_op jit(solution)/shard_map/div | solution.py:90
  145.0 2.5 %copy.30 = f32[48,48,128]{2,1,0:T(8,128)S(1)} copy(f32[48,48,128]{1,2,0:T(8,128)} %bitcast.85) | data formatting | bytes 2359296 | tf_op jit(solution)/shard_map/reshape | solution.py:26
  147.6 1.5 %convolution_convert_fusion.2 = bf16[48,48,128]{2,1,0:T(8,128)(2,1)} fusion(bf16[48,48,128]{2,1,0:T(8,128)(2,1)S(1)} %copy-done.3, f32[48,48,128]{2,1,0:T(8,128)S(1)} %copy.30, f32[48,48,128]{2,1,0:T(8,128)S(1)} %copy-done.6, bf16[128,128]{1,0:T(8,128)(2,1)S(1)} %copy-done.12, bf16[128,128]{1,0:T(8,128)(2,1)S(1)} %copy-done.13), kind=kOutput, calls=%fused_computation.37 | convolution fusion | flops 153059328 | bytes 3604480 | tf_op jit(solution)/shard_map/dot_general | solution.py:93
  (105 shorter events, 30.7 us)
Async XLA Ops:
  0.0 86.4 %copy-start = (bf16[128,128]{1,0:T(8,128)(2,1)S(1)}, bf16[128,128]{1,0:T(8,128)(2,1)}, u32[]{:S(2)}) copy-start(bf16[128,128]{1,0:T(8,128)(2,1)} %param.12) | copy-start | bytes 98308
  0.0 74.2 %copy-start.10 = (bf16[4,48,96]{2,1,0:T(8,128)(2,1)S(1)}, bf16[4,48,96]{2,1,0:T(8,128)(2,1)}, u32[]{:S(2)}) copy-start(bf16[4,48,96]{2,1,0:T(8,128)(2,1)} %param.17) | copy-start | bytes 110596
  3.3 0.6 copy-start.7
  5.6 84.3 %copy-start.2 = (bf16[48,48,128]{2,1,0:T(8,128)(2,1)}, bf16[48,48,128]{2,1,0:T(8,128)(2,1)S(1)}, u32[]{:S(2)}) copy-start(bf16[48,48,128]{2,1,0:T(8,128)(2,1)S(1)} %fusion.27) | copy-start | bytes 1769476
  5.6 12.1 %collective-permute-start = (bf16[48,48,128]{2,1,0:T(8,128)(2,1)S(1)}, bf16[48,48,128]{2,1,0:T(8,128)(2,1)S(1)}, u32[]{:S(2)}, u32[]{:S(2)}) collective-permute-start(bf16[48,48,128]{2,1,0:T(8,128)(2,1)S(1)} %fusion.27), channel_id=1, source_target_pairs={{0,1},{1,2},{2,3},{3,4},{4,5},{5,6},{6,7},{7,0},{8,9},{9,10},{10,1... | collective-permute-start | bytes 1769480 | tf_op jit(solution)/shard_map/ppermute | solution.py:71
  17.8 11.1 %collective-permute-start.1 = (bf16[48,48,128]{2,1,0:T(8,128)(2,1)S(1)}, bf16[48,48,128]{2,1,0:T(8,128)(2,1)S(1)}, u32[]{:S(2)}, u32[]{:S(2)}) collective-permute-start(bf16[48,48,128]{2,1,0:T(8,128)(2,1)S(1)} %collective-permute-done), channel_id=1, source_target_pairs={{0,1},{1,2},{2,3},{3,4},{4,5},{5,6},{6,7},{7,0},{8,9},{9,10},{10,1... | collective-permute-start | bytes 1769480 | tf_op jit(solution)/shard_map/ppermute | solution.py:71
  28.9 11.1 %collective-permute-start.2 = (bf16[48,48,128]{2,1,0:T(8,128)(2,1)S(1)}, bf16[48,48,128]{2,1,0:T(8,128)(2,1)S(1)}, u32[]{:S(2)}, u32[]{:S(2)}) collective-permute-start(bf16[48,48,128]{2,1,0:T(8,128)(2,1)S(1)} %collective-permute-done.1), channel_id=1, source_target_pairs={{0,1},{1,2},{2,3},{3,4},{4,5},{5,6},{6,7},{7,0},{8,9},{9,10},{10,1... | collective-permute-start | bytes 1769480 | tf_op jit(solution)/shard_map/ppermute | solution.py:71
  40.0 11.1 %collective-permute-start.3 = (bf16[48,48,128]{2,1,0:T(8,128)(2,1)S(1)}, bf16[48,48,128]{2,1,0:T(8,128)(2,1)S(1)}, u32[]{:S(2)}, u32[]{:S(2)}) collective-permute-start(bf16[48,48,128]{2,1,0:T(8,128)(2,1)S(1)} %collective-permute-done.2), channel_id=1, source_target_pairs={{0,1},{1,2},{2,3},{3,4},{4,5},{5,6},{6,7},{7,0},{8,9},{9,10},{10,1... | collective-permute-start | bytes 1769480 | tf_op jit(solution)/shard_map/ppermute | solution.py:71
  51.1 11.1 %collective-permute-start.4 = (bf16[48,48,128]{2,1,0:T(8,128)(2,1)S(1)}, bf16[48,48,128]{2,1,0:T(8,128)(2,1)S(1)}, u32[]{:S(2)}, u32[]{:S(2)}) collective-permute-start(bf16[48,48,128]{2,1,0:T(8,128)(2,1)S(1)} %collective-permute-done.3), channel_id=1, source_target_pairs={{0,1},{1,2},{2,3},{3,4},{4,5},{5,6},{6,7},{7,0},{8,9},{9,10},{10,1... | collective-permute-start | bytes 1769480 | tf_op jit(solution)/shard_map/ppermute | solution.py:71
  62.2 0.8 copy-start.4
  63.0 11.2 %collective-permute-start.5 = (bf16[48,48,128]{2,1,0:T(8,128)(2,1)S(1)}, bf16[48,48,128]{2,1,0:T(8,128)(2,1)}, u32[]{:S(2)}, u32[]{:S(2)}) collective-permute-start(bf16[48,48,128]{2,1,0:T(8,128)(2,1)S(1)} %collective-permute-done.4), channel_id=1, source_target_pairs={{0,1},{1,2},{2,3},{3,4},{4,5},{5,6},{6,7},{7,0},{8,9},{9,10},{10,1... | collective-permute-start | bytes 1769480 | tf_op jit(solution)/shard_map/ppermute | solution.py:71
  74.2 13.4 %collective-permute-start.6 = (bf16[48,48,128]{2,1,0:T(8,128)(2,1)}, bf16[48,48,128]{2,1,0:T(8,128)(2,1)}, u32[]{:S(2)}, u32[]{:S(2)}) collective-permute-start(bf16[48,48,128]{2,1,0:T(8,128)(2,1)} %collective-permute-done.5), channel_id=1, source_target_pairs={{0,1},{1,2},{2,3},{3,4},{4,5},{5,6},{6,7},{7,0},{8,9},{9,10},{10,1... | collective-permute-start | bytes 1769480 | tf_op jit(solution)/shard_map/ppermute | solution.py:71
  86.4 3.5 %copy-start.5 = (bf16[48,48,128]{2,1,0:T(8,128)(2,1)S(1)}, bf16[48,48,128]{2,1,0:T(8,128)(2,1)}, u32[]{:S(2)}) copy-start(bf16[48,48,128]{2,1,0:T(8,128)(2,1)} %copy-done.4) | copy-start | bytes 1769476
  90.0 1.1 copy-start.1
  90.0 1.1 copy-start.8
  90.0 1.1 copy-start.11
  95.8 4.2 %copy-start.9 = (f32[6,8,4,48]{3,2,1,0:T(4,128)S(1)}, f32[6,8,4,48]{3,2,1,0:T(4,128)}, u32[]{:S(2)}) copy-start(f32[6,8,4,48]{3,2,1,0:T(4,128)} %custom-call.1) | copy-start | bytes 110596
  145.0 2.5 %copy-start.3 = (bf16[48,48,128]{2,1,0:T(8,128)(2,1)S(1)}, bf16[48,48,128]{2,1,0:T(8,128)(2,1)}, u32[]{:S(2)}) copy-start(bf16[48,48,128]{2,1,0:T(8,128)(2,1)} %copy-done.2) | copy-start | bytes 1769476
  145.0 2.5 %copy-start.6 = (f32[48,48,128]{2,1,0:T(8,128)S(1)}, f32[48,48,128]{2,1,0:T(8,128)}, u32[]{:S(2)}) copy-start(f32[48,48,128]{2,1,0:T(8,128)} %copy.31) | copy-start | bytes 3538948
  145.0 2.5 %copy-start.12 = (bf16[128,128]{1,0:T(8,128)(2,1)S(1)}, bf16[128,128]{1,0:T(8,128)(2,1)}, u32[]{:S(2)}) copy-start(bf16[128,128]{1,0:T(8,128)(2,1)} %param.16) | copy-start | bytes 98308
  145.0 2.5 %copy-start.13 = (bf16[128,128]{1,0:T(8,128)(2,1)S(1)}, bf16[128,128]{1,0:T(8,128)(2,1)}, u32[]{:S(2)}) copy-start(bf16[128,128]{1,0:T(8,128)(2,1)} %param.15) | copy-start | bytes 98308
